TPU v7x, 128 devices: a whole 4x4x4 slice. The times are simulated.
128 devices in a mesh: tmpl: 2 (over core), row: 16 (over y, z), col: 4 (over x).
Axes of the slice: x: 4, y: 4, z: 4, core: 2. Of those that a mesh axis runs over, the one named last changes fastest.
Arguments:
- template_pair: bfloat16 [2, 512, 64, 512], P('tmpl', 'row', None, 'col'), may hold values from -6 to 6
- trunk: bfloat16 [512, 128, 512], P('row', None, 'col'), may hold values from -6 to 6
- coverage: int32 [2, 512], replicated, may hold values from 0 to 1, as said below
- chain_ids: int32 [512], replicated, may hold values from 0 to 3, never falling along the last dimension, each value on 1 to 256 neighbouring positions
- chain_vec: float32 [64], replicated, may hold values from -4 to 4
- trunk_weights: bfloat16 [64, 128], replicated, may hold values from -0.5 to 0.5
- proj_weights: bfloat16 [2, 5, 64, 64], replicated, may hold values from -0.75 to 0.75
- out_weights: bfloat16 [2, 64, 64], replicated, may hold values from -0.75 to 0.75
- final_weights: bfloat16 [128, 64], replicated, may hold values from -0.75 to 0.75
Outputs:
- trunk_out: bfloat16 [512, 128, 512], P('row', None, 'col')
Inputs may be any that keep to these rules, and one draw needn't show every extreme that they name: coverage[t, i] is 1 where template t covers token i, else 0; how densely a template covers tokens is drawn anew for each block of 32 consecutive tokens. `chain_ids`: chain ids never fall along the tokens.
All inputs are finite; a program needn't handle non-finite values.
Results may differ from a plain program's by a relative error of at most 0.008.
Values may be sent and summed in bfloat16 or wider, within the bound.
A program may use at most 128 MiB of HBM per device.

v0:
```python
import jax
import jax.numpy as jnp
from jax import lax
from jax.sharding import PartitionSpec as P

epsilon = 1e-05


def in_blocks(array, dim, count):
    lengths = array.shape
    parts = array.reshape(*lengths[:dim], count, lengths[dim] // count, *lengths[dim + 1 :])
    return jnp.moveaxis(parts, dim, 0)


def sent_and_summed(array, axis, dim):
    parts = in_blocks(array, dim, lax.axis_size(axis))
    arrived = lax.all_to_all(parts, axis, split_axis=0, concat_axis=0, tiled=True)
    return arrived.astype(jnp.float32).sum(axis=0)


def sent_to_all(array, axis):
    copies = jnp.broadcast_to(array, (lax.axis_size(axis), *array.shape))
    return lax.all_to_all(copies, axis, split_axis=0, concat_axis=0, tiled=True)


def joined_along(parts, dim):
    parts = jnp.moveaxis(parts, 0, dim)
    lengths = parts.shape
    return parts.reshape(*lengths[:dim], lengths[dim] * lengths[dim + 1], *lengths[dim + 2 :])


def gathered_copies(array, axis, dim):
    parts = sent_to_all(array, axis)
    return joined_along(parts, dim)


def over_copies(array, axis):
    return sent_to_all(array, axis).astype(jnp.float32).sum(axis=0)


def channel_norm(values):
    centre = jnp.mean(values, axis=1, keepdims=True)
    centred = values - centre
    spread = jnp.mean(centred * centred, axis=1, keepdims=True)
    return centred * lax.rsqrt(spread + epsilon)


def project(weights, values):
    return jnp.einsum("dc,icj->idj", weights, values, preferred_element_type=jnp.float32)


def gated_pair(pair_rep, pair_mask, weights):
    channels = pair_rep.shape[1]
    normed = channel_norm(pair_rep.astype(jnp.float32)).astype(jnp.bfloat16)
    stacked = project(weights.reshape(5 * channels, channels), normed)
    pieces = [stacked[:, number * channels : (number + 1) * channels, :] for number in range(5)]
    weighted = pair_mask[:, None, :]
    left_proj = (weighted * jax.nn.sigmoid(pieces[0]) * pieces[1]).astype(jnp.bfloat16)
    right_proj = (weighted * jax.nn.sigmoid(pieces[2]) * pieces[3]).astype(jnp.bfloat16)
    return (left_proj, right_proj, pieces[4])


def apply_update(pair_rep, tri_sum, gate_proj, weights):
    tri_norm = channel_norm(tri_sum).astype(jnp.bfloat16)
    update = jax.nn.sigmoid(gate_proj) * project(weights, tri_norm)
    return (pair_rep.astype(jnp.float32) + update).astype(jnp.bfloat16)


def outgoing(left_proj, right_proj):
    right_cols = lax.all_gather(right_proj, "row", axis=0, tiled=True)
    partial_value = jnp.einsum(
        "ick,jck->icj", left_proj, right_cols, preferred_element_type=jnp.float32
    )
    return sent_and_summed(partial_value.astype(jnp.bfloat16), "col", 2)


def incoming(left_proj, right_proj):
    left_rows = gathered_copies(left_proj, "col", 2)
    return lax.psum_scatter(
        jnp.einsum(
            "kci,kcj->icj", left_rows, right_proj, preferred_element_type=jnp.float32
        ).astype(jnp.bfloat16),
        "row",
        scatter_dimension=0,
        tiled=True,
    ).astype(jnp.float32)


def finish(trunk, pooled, cover_count, final_weights):
    hidden = jax.nn.relu(pooled / jnp.maximum(cover_count, 1.0)[:, None, :]).astype(jnp.bfloat16)
    return (trunk.astype(jnp.float32) + project(final_weights, hidden)).astype(jnp.bfloat16)


def per_device(
    template_pair,
    trunk,
    coverage,
    chain_ids,
    chain_vec,
    trunk_weights,
    proj_weights,
    out_weights,
    final_weights,
):
    tile_rows, trunk_channels, tile_cols = trunk.shape
    row_start = lax.axis_index("row") * tile_rows
    col_start = lax.axis_index("col") * tile_cols
    cover_float = coverage.astype(jnp.float32)
    cover_rows = lax.dynamic_slice_in_dim(cover_float, row_start, tile_rows, 1)
    cover_cols = lax.dynamic_slice_in_dim(cover_float, col_start, tile_cols, 1)
    cover_count = jnp.sum(cover_rows[:, :, None] * cover_cols[:, None, :], axis=0)
    chain_rows = lax.dynamic_slice_in_dim(chain_ids, row_start, tile_rows, 0)
    chain_cols = lax.dynamic_slice_in_dim(chain_ids, col_start, tile_cols, 0)
    same_chain = (chain_rows[:, None] == chain_cols[None, :]).astype(jnp.float32)
    trunk_proj = project(trunk_weights, channel_norm(trunk.astype(jnp.float32)))
    local_templates = template_pair.shape[0]
    template_index = lax.axis_index("tmpl") * local_templates + 0
    mask_rows = lax.dynamic_index_in_dim(cover_rows, template_index, 0, keepdims=False)
    mask_cols = lax.dynamic_index_in_dim(cover_cols, template_index, 0, keepdims=False)
    pair_mask = mask_rows[:, None] * mask_cols[None, :]
    pair_rep = (
        template_pair[0].astype(jnp.float32)
        + same_chain[:, None, :] * chain_vec[None, :, None]
        + trunk_proj
    ).astype(jnp.bfloat16)
    left_proj, right_proj, gate_proj = gated_pair(pair_rep, pair_mask, proj_weights[0])
    pair_rep = apply_update(pair_rep, outgoing(left_proj, right_proj), gate_proj, out_weights[0])
    left_proj, right_proj, gate_proj = gated_pair(pair_rep, pair_mask, proj_weights[1])
    pair_rep = apply_update(pair_rep, incoming(left_proj, right_proj), gate_proj, out_weights[1])
    pooled = pair_mask[:, None, :] * channel_norm(pair_rep.astype(jnp.float32))
    pooled_all = over_copies(pooled.astype(jnp.bfloat16), "tmpl").astype(jnp.float32)
    return finish(trunk, pooled_all, cover_count, final_weights)


def solution(mesh):
    in_specs = (
        P("tmpl", "row", None, "col"),
        P("row", None, "col"),
        P(),
        P(),
        P(),
        P(),
        P(),
        P(),
        P(),
    )
    out_specs = P("row", None, "col")
    return jax.shard_map(
        per_device, mesh=mesh, in_specs=in_specs, out_specs=out_specs, check_vma=False
    )
```

profile of v0, /device:TPU:1, one launch (start us, length us, event | category | flops | bytes accessed | tf_op | source)
XLA Modules:
  0.0 298.9 jit_solution(2865312814107354440)
XLA Ops:
  6.5 0.8 dynamic_slice.22
  7.3 0.8 dynamic_slice.23
  8.1 1.7 copy.80
  9.7 0.3 convert_reduce_fusion.2
  10.1 1.3 fusion.4
  11.5 1.6 convert_reduce_fusion.5
  13.6 0.8 convolution_bitcast_fusion.1
  14.5 1.9 fusion.55
  16.4 0.6 copy-done.2
  17.2 73.9 %all-gather.2.cloned.1.call-done = bf16[512,64,128]{2,1,0:T(8,128)(2,1)} async-done(((bf16[32,64,128]{2,1,0:T(8,128)(2,1)}), bf16[512,64,128]{2,1,0:T(8,128)(2,1)}) %all-gather.2.cloned.1.call-update) | async-done | bytes 8388624 | tf_op jit(solution)/shard_map/all_gather | solution.py:70
  91.1 21.2 %convert_bitcast_fusion.1 = bf16[64,4,4,8,128]{4,3,2,1,0:T(8,128)(2,1)S(1)} fusion(bf16[512,64,128]{2,1,0:T(8,128)(2,1)} %all-gather.2.cloned.1.call-done, bf16[32,64,128]{2,1,0:T(8,128)(2,1)S(1)} %get-tuple-element.9), kind=kOutput, calls=%fused_computation.19 | convolution fusion | flops 269484032 | bytes 11010048 | tf_op jit(solution)/shard_map/ick,jck->icj/dot_general | solution.py:71
  112.4 0.4 copy.125
  112.8 29.1 %all_to_all.15 = bf16[4,32,64,128]{3,1,2,0:T(8,128)(2,1)S(1)} all-to-all(bf16[4,32,64,128]{3,1,2,0:T(8,128)(2,1)S(1)} %bitcast.82), channel_id=1, replica_groups=mesh['tmpl'=2,'row'=16,'col'=4] {'col'}, dimensions={0} | all-to-all | bytes 4194304 | tf_op jit(solution)/shard_map/all_to_all | solution.py:17
  141.9 0.9 convert_reduce_fusion
  143.1 0.4 copy-done.6
  143.5 1.8 convert_reduce_fusion.4
  145.5 0.8 convolution_bitcast_fusion
  146.4 0.6 fusion.47
  147.0 1.7 copy-done.1
  148.7 0.3 copy.89
  149.0 0.3 broadcast_in_dim.4
  149.4 26.9 %all_to_all.16 = bf16[4,32,64,128]{3,1,2,0:T(8,128)(2,1)S(1)} all-to-all(bf16[4,32,64,128]{3,1,2,0:T(8,128)(2,1)S(1)} %broadcast_in_dim.4), channel_id=1, replica_groups=mesh['tmpl'=2,'row'=16,'col'=4] {'col'}, dimensions={0} | all-to-all | bytes 4194304 | tf_op jit(solution)/shard_map/all_to_all | solution.py:23
  176.3 5.6 %convert_bitcast_fusion = bf16[512,64,128]{0,2,1:T(8,128)(2,1)} fusion(bf16[32,64,128]{2,1,0:T(8,128)(2,1)S(1)} %get-tuple-element.7, bf16[4,32,64,128]{3,1,2,0:T(8,128)(2,1)S(1)} %all_to_all.16), kind=kOutput, calls=%fused_computation.2 | convolution fusion | flops 272629760 | bytes 11010048 | tf_op jit(solution)/shard_map/kci,kcj->icj/dot_general | solution.py:80
  181.9 12.0 %copy.92 = bf16[512,64,128]{2,1,0:T(8,128)(2,1)} copy(bf16[512,64,128]{0,2,1:T(8,128)(2,1)} %convert_bitcast_fusion) | data formatting | bytes 16777216 | tf_op jit(solution)/shard_map/convert_element_type | solution.py:82
  194.1 84.5 %reduce-scatter.2.cloned.1.call-done = bf16[32,64,128]{2,1,0:T(8,128)(2,1)} async-done(((bf16[512,64,128]{2,1,0:T(8,128)(2,1)}), bf16[32,64,128]{2,1,0:T(8,128)(2,1)}) %reduce-scatter.2.cloned.1.call-update) | async-done | bytes 524304 | tf_op jit(solution)/shard_map/reduce_scatter | solution.py:79
  278.6 1.1 convert_reduce_fusion.7
  279.8 1.2 fusion.40
  281.0 1.9 convert_reduce_fusion.6
  283.4 0.3 broadcast_in_dim.5
  283.7 6.3 %all_to_all.17 = bf16[2,32,64,128]{3,2,1,0:T(8,128)(2,1)S(1)} all-to-all(bf16[2,32,64,128]{3,2,1,0:T(8,128)(2,1)S(1)} %broadcast_in_dim.5), channel_id=1, replica_groups=mesh['tmpl'=2,'row'=16,'col'=4] {'tmpl'}, dimensions={0} | all-to-all | bytes 2097152 | tf_op jit(solution)/shard_map/all_to_all | solution.py:23
  290.2 0.5 fusion.7
  290.7 1.3 copy.97
  (48 shorter events, 2.1 us)
Async XLA Ops:
  6.5 283.7 %copy-start = (bf16[128,64]{0,1:T(8,128)(2,1)S(1)}, bf16[128,64]{0,1:T(8,128)(2,1)}, u32[]{:S(2)}) copy-start(bf16[128,64]{0,1:T(8,128)(2,1)} %param.17) | copy-start | bytes 49156
  6.5 84.6 %all-gather.2.cloned.1.call-start = ((), (), s32[]{:S(2)}) async-start(), calls=%async_computation.4 | async-start | bytes 8912896 | tf_op jit(solution)/shard_map/all_gather | solution.py:70
  8.1 3.5 %copy-start.5 = (bf16[1,32,64,128]{3,2,1,0:T(8,128)(2,1)S(1)}, bf16[1,32,64,128]{3,2,1,0:T(8,128)(2,1)}, u32[]{:S(2)}) copy-start(bf16[1,32,64,128]{3,2,1,0:T(8,128)(2,1)} %param.9) | copy-start | bytes 1572868
  8.1 3.5 %copy-start.7 = (bf16[64,128]{1,0:T(8,128)(2,1)S(1)}, bf16[64,128]{1,0:T(8,128)(2,1)}, u32[]{:S(2)}) copy-start(bf16[64,128]{1,0:T(8,128)(2,1)} %param.14) | copy-start | bytes 49156
  8.1 3.5 %copy-start.8 = (f32[64]{0:T(128)S(1)}, f32[64]{0:T(128)}, u32[]{:S(2)}) copy-start(f32[64]{0:T(128)} %param.13) | copy-start | bytes 772
  11.4 2.0 copy-start.3
  11.5 1.9 copy-start.4
  14.4 2.6 copy-start.2
  17.0 261.6 %reduce-scatter.2.cloned.1.call-start = ((), (), s32[]{:S(2)}) async-start(), calls=%async_computation.5 | async-start | bytes 8912896 | tf_op jit(solution)/shard_map/reduce_scatter | solution.py:79
  142.8 0.8 copy-start.6
  146.4 2.3 copy-start.1
Sparse Core Ops, SparseCore 0:
  17.1 73.9 all-gather.1
  194.1 84.5 reduce-scatter.1
where the time goes:
time: 300 us; the launch traced here: 299 us
  waiting for transfers between devices  158 us (53%)
  blocking collectives  62.3 us (21%)
  matrix products  34.3 us (11%)
  local copies, waits for them, and re-layouts  20.8 us (7%)
  between operations  13.7 us (5%)
  other arithmetic  9.03 us (3%)
    reduce_scatter x1, waiting for transfers between devices, incoming(): lax.psum_scatter(jnp.einsum('kci,kcj->icj', left_rows, right_proj, prefer...  84.5 us
    all_gather x1, waiting for transfers between devices, outgoing(): right_cols = lax.all_gather(right_proj, 'row', axis=0, tiled=True)  73.9 us
    all_to_all x2, blocking collectives, sent_to_all(): return lax.all_to_all(copies, axis, split_axis=0, concat_axis=0, tiled=True)  33.2 us
    all_to_all x1, blocking collectives, sent_and_summed(): lax.all_to_all(parts, axis, split_axis=0, concat_axis=0, tiled=True)  29.1 us
    dot_general x1, matrix products, outgoing(): jnp.einsum('ick,jck->icj', left_proj, right_cols, preferred_element_type=...  21.2 us
    convert_element_type x1, local copies, waits for them, and re-layouts, incoming(): return lax.psum_scatter(jnp.einsum('kci,kcj->icj', left_rows, right_proj,...  12 us
    dot_general x6, matrix products, project(): jnp.einsum('dc,icj->idj', weights, values, preferred_element_type=jnp.flo...  7.5 us
  transfers between devices with their start and end apart: 2, of which 2 were waited for; matrix products, arithmetic and copies ran while one was open for 0% of the time, Pallas kernels for 0%

commit v1 on v0

v1 whole, which is shorter than its diff:
```python
import functools

import jax
import jax.numpy as jnp
from jax import lax
from jax.experimental import pallas as pl
from jax.experimental.pallas import tpu as pltpu
from jax.sharding import PartitionSpec as P

MESH = pl.DeviceIdType.MESH
EPS = 1e-05
F32 = jnp.float32
BF16 = jnp.bfloat16
ROWS, COLS, C, CZ = 32, 128, 64, 128
HALF = 16
DEV = 64


def dot(a, b):
    return jnp.dot(a, b, preferred_element_type=F32)


def iota(shape, dim):
    return lax.broadcasted_iota(jnp.int32, shape, dim)


def to_rhs(x):
    a = x[:, 0:8].reshape(512, COLS).astype(BF16)
    b = x[:, 8:16].reshape(512, COLS).astype(BF16)
    return jnp.concatenate([a, b], axis=1)


def from_out(o):
    a = o[:, 0:COLS].reshape(C, 8, COLS)
    b = o[:, COLS:].reshape(C, 8, COLS)
    return jnp.concatenate([a, b], axis=1)


def norm0(x):
    centred = x - jnp.mean(x, axis=0, keepdims=True)
    spread = jnp.mean(centred * centred, axis=0, keepdims=True)
    return centred * lax.rsqrt(spread + EPS)


def sigmoid(x):
    return 0.5 * jnp.tanh(0.5 * x) + 0.5


def kron_rows():
    return (iota((512, C), 0) // 8 == iota((512, C), 1)).astype(BF16)


def kron_cols():
    return (iota((C, 512), 1) // 8 == iota((C, 512), 0)).astype(BF16)


def kron8(w):
    tall = dot(kron_rows(), w).astype(BF16)
    full = dot(tall, kron_cols())
    same = lax.rem(iota((512, 512), 0), 8) == lax.rem(iota((512, 512), 1), 8)
    return jnp.where(same, full, 0.0).astype(BF16)


def kernel(
    tp_hbm, trunk_hbm, cover_ref, chain_ref, vec_ref, wt_ref, wp_ref, wo_ref, wf_ref,
    out_hbm,
    tp_v, tr_v, out_v, k_perm, k_trunk, k_proj, k_out, k_final,
    pair_v, normed_v, gate_v, sbuf, rbuf, tsend, tbuf, psend, pbuf,
    ld_sem, st_sem, own_sem, ssem, rsem, tssem, trsem, pssem, prsem,
):
    tmpl = lax.axis_index("tmpl")
    row = lax.axis_index("row")
    x = lax.axis_index("col")
    y, z = lax.div(row, 4), lax.rem(row, 4)
    me = x * 16 + row

    load_tp = pltpu.make_async_copy(tp_hbm.at[0], tp_v, ld_sem.at[0])
    load_tr = pltpu.make_async_copy(trunk_hbm, tr_v, ld_sem.at[1])
    load_tp.start()
    load_tr.start()

    def peer(step):
        mixed = lax.rem(step * 29, DEV)
        px = lax.rem(x + lax.rem(mixed, 4), 4)
        py = lax.rem(y + lax.rem(lax.div(mixed, 4), 4), 4)
        pz = lax.rem(z + lax.div(mixed, 16), 4)
        prow = py * 4 + pz
        return prow, px, px * 16 + prow

    barrier = pltpu.get_barrier_semaphore()

    def greet(step, carry):
        prow, pcol, _ = peer(step)
        pl.semaphore_signal(
            barrier, inc=1, device_id=(tmpl, prow, pcol), device_id_type=MESH
        )
        return carry

    lax.fori_loop(1, DEV, greet, 0)
    pl.semaphore_signal(barrier, inc=1, device_id=(1 - tmpl, row, x), device_id_type=MESH)

    def send_all(source, target, send_sem, recv_sem):
        def send(step, carry):
            prow, pcol, number = peer(step)
            pltpu.make_async_remote_copy(
                src_ref=source(number), dst_ref=target, send_sem=send_sem, recv_sem=recv_sem,
                device_id=(tmpl, prow, pcol), device_id_type=MESH,
            ).start()
            return carry

        lax.fori_loop(1, DEV, send, 0)

    def wait_all(view, sem):
        pltpu.make_async_copy(view, view, sem).wait()

    def part(ref, number, h):
        return ref.at[number, :, pl.ds(h * HALF, HALF), :]

    cover = cover_ref[...].astype(F32)
    picks = (iota((ROWS, 512), 1) == row * ROWS + iota((ROWS, 512), 0)).astype(BF16)

    def row_plane(line):
        spread = jnp.broadcast_to(line, (COLS, 512)).astype(BF16)
        return lax.dot_general(picks, spread, (((1,), (1,)), ((), ())), preferred_element_type=F32)

    lanes = pl.ds(pl.multiple_of(x * COLS, COLS), COLS)
    cols_of = cover_ref[:, lanes].astype(F32)
    masks = [row_plane(cover[t : t + 1]) * cols_of[t : t + 1] for t in range(2)]
    mask = jnp.where(tmpl == 0, masks[0], masks[1])
    count = jnp.maximum(masks[0] + masks[1], 1.0)
    chain_rows = row_plane(chain_ref[...].astype(F32))
    same_chain = jnp.where(chain_rows == chain_ref[:, lanes].astype(F32), 1.0, 0.0)

    left_row, left_col = iota((512, 512), 0), iota((512, 512), 1)
    k_perm[...] = jnp.where(
        (lax.div(left_row, 8) == lax.rem(left_col, C)) & (lax.rem(left_row, 8) == lax.div(left_col, C)),
        1.0, 0.0,
    ).astype(BF16)
    tall_trunk = dot(kron_rows(), wt_ref[...])
    for i in range(8):
        keep = lax.rem(iota((512, CZ), 0), 8) == i
        k_trunk[:, i * CZ : (i + 1) * CZ] = jnp.where(keep, tall_trunk, 0.0).astype(BF16)
    for d in range(4):
        k_proj[0, d] = kron8(wp_ref[0, d])

    def products(m, h):
        rhs = normed_v[h]
        plane = mask[h * HALF : (h + 1) * HALF][None]
        for side in range(2):
            gate = from_out(dot(k_proj[m, 2 * side], rhs))
            value = from_out(dot(k_proj[m, 2 * side + 1], rhs))
            sbuf[m, :, side, h * HALF : (h + 1) * HALF, :] = (plane * sigmoid(gate) * value).astype(BF16)

    def gates(m, h):
        gate_v[h] = sigmoid(from_out(dot(k_proj[m, 4], normed_v[h])))

    def updated(m, h, tri):
        tri_norm = to_rhs(norm0(tri))
        update = gate_v[h] * from_out(dot(k_out[m], tri_norm))
        return (pair_v[h].astype(F32) + update).astype(BF16)

    load_tp.wait()
    load_tr.wait()
    for h in range(2):
        lo = h * HALF
        tr = tr_v[lo : lo + HALF].astype(F32)
        centred = tr - jnp.mean(tr, axis=1, keepdims=True)
        spread = jnp.mean(centred * centred, axis=1, keepdims=True)
        trn = (centred * lax.rsqrt(spread + EPS)).astype(BF16)
        rhs = jnp.concatenate(
            [trn[0:8].reshape(8 * CZ, COLS), trn[8:16].reshape(8 * CZ, COLS)], axis=1
        )
        pair = from_out(dot(k_trunk[...], rhs))
        tp = tp_v[lo : lo + HALF]
        rhs = jnp.concatenate([tp[0:8].reshape(512, COLS), tp[8:16].reshape(512, COLS)], axis=1)
        pair = pair + from_out(dot(k_perm[...], rhs))
        pair = pair + same_chain[lo : lo + HALF][None] * vec_ref[...]
        pair = pair.astype(BF16)
        pair_v[h] = pair
        normed_v[h] = to_rhs(norm0(pair.astype(F32)))
        products(0, h)
        if h == 0:
            pl.semaphore_wait(barrier, DEV)
        send_all(lambda n: part(sbuf.at[0], n, h), part(rbuf.at[0], me, h), ssem.at[0, h], rsem.at[0, h])
        pltpu.make_async_copy(part(sbuf.at[0], me, h), part(rbuf.at[0], me, h), own_sem.at[0, h]).start()

    k_proj[0, 4] = kron8(wp_ref[0, 4])
    for h in range(2):
        gates(0, h)
    for m in range(2):
        k_out[m] = kron8(wo_ref[m])
    for d in range(5):
        k_proj[1, d] = kron8(wp_ref[1, d])
    wide = dot(wf_ref[...], kron_cols())
    for i in range(8):
        keep = lax.rem(iota((CZ, 512), 1), 8) == i
        k_final[i * CZ : (i + 1) * CZ, :] = jnp.where(keep, wide, 0.0).astype(BF16)

    def wait_products(m):
        for h in range(2):
            view = rbuf.at[m, pl.ds(0, DEV - 1), :, pl.ds(h * HALF, HALF), :]
            wait_all(view, rsem.at[m, h])
            pltpu.make_async_copy(part(sbuf.at[m], me, h), part(rbuf.at[m], me, h), own_sem.at[m, h]).wait()

    def gathered(m, side):
        return jnp.concatenate(
            [rbuf[m, q * 16 : (q + 1) * 16, side].reshape(512, COLS) for q in range(4)], axis=1
        )

    wait_products(0)
    right = gathered(0, 1)
    for h in range(2):
        lo = h * HALF
        left = jnp.concatenate(
            [rbuf[0, q * 16 : (q + 1) * 16, 0, lo : lo + HALF].reshape(256, COLS) for q in range(4)],
            axis=1,
        )
        tri = lax.dot_general(left, right, (((1,), (1,)), ((), ())), preferred_element_type=F32)
        for q in range(4):
            tsend[0, q * 16 : (q + 1) * 16, lo : lo + HALF, :] = (
                tri[:, q * COLS : (q + 1) * COLS].reshape(16, HALF, COLS).astype(BF16)
            )
        rows_of = pl.ds(lo, HALF)
        send_all(
            lambda n: tsend.at[0, n, rows_of, :], tbuf.at[0, me, rows_of, :],
            tssem.at[0, h], trsem.at[0, h],
        )
        pltpu.make_async_copy(
            tsend.at[0, me, rows_of, :], tbuf.at[0, me, rows_of, :], own_sem.at[2, h]
        ).start()
    for h in range(2):
        lo = h * HALF
        rows_of = pl.ds(lo, HALF)
        wait_all(tbuf.at[0, pl.ds(0, DEV - 1), rows_of, :], trsem.at[0, h])
        pltpu.make_async_copy(
            tsend.at[0, me, rows_of, :], tbuf.at[0, me, rows_of, :], own_sem.at[2, h]
        ).wait()
        pair = updated(0, h, tbuf[0, :, lo : lo + HALF, :].astype(F32))
        pair_v[h] = pair
        normed_v[h] = to_rhs(norm0(pair.astype(F32)))
        products(1, h)
        send_all(lambda n: part(sbuf.at[1], n, h), part(rbuf.at[1], me, h), ssem.at[1, h], rsem.at[1, h])
        pltpu.make_async_copy(part(sbuf.at[1], me, h), part(rbuf.at[1], me, h), own_sem.at[1, h]).start()
    for h in range(2):
        gates(1, h)

    wait_products(1)
    right = gathered(1, 1)
    tri = lax.dot_general(gathered(1, 0), right, (((0,), (0,)), ((), ())), preferred_element_type=F32)
    for q in range(4):
        tsend[1, q * 16 : (q + 1) * 16, :, :] = (
            tri[:, q * COLS : (q + 1) * COLS].reshape(16, ROWS, COLS).astype(BF16)
        )
    for h in range(2):
        rows_of = pl.ds(h * HALF, HALF)
        send_all(
            lambda n: tsend.at[1, n, rows_of, :], tbuf.at[1, me, rows_of, :],
            tssem.at[1, h], trsem.at[1, h],
        )
        pltpu.make_async_copy(
            tsend.at[1, me, rows_of, :], tbuf.at[1, me, rows_of, :], own_sem.at[3, h]
        ).start()

    def across(h):
        return pltpu.make_async_remote_copy(
            src_ref=psend.at[h], dst_ref=pbuf.at[h], send_sem=pssem.at[h], recv_sem=prsem.at[h],
            device_id=(1 - tmpl, row, x), device_id_type=MESH,
        )

    for h in range(2):
        lo = h * HALF
        rows_of = pl.ds(lo, HALF)
        wait_all(tbuf.at[1, pl.ds(0, DEV - 1), rows_of, :], trsem.at[1, h])
        pltpu.make_async_copy(
            tsend.at[1, me, rows_of, :], tbuf.at[1, me, rows_of, :], own_sem.at[3, h]
        ).wait()
        pair = updated(1, h, tbuf[1, :, lo : lo + HALF, :].astype(F32))
        pooled = mask[lo : lo + HALF][None] * norm0(pair.astype(F32))
        psend[h] = pooled.astype(BF16)
        across(h).start()
    for h in range(2):
        lo = h * HALF
        across(h).wait_recv()
        pooled = psend[h].astype(F32) + pbuf[h].astype(F32)
        hidden = jnp.maximum(pooled / count[lo : lo + HALF][None], 0.0)
        out = dot(k_final[...], to_rhs(hidden))
        for side in range(2):
            first = lo + 8 * side
            block = out[:, side * COLS : (side + 1) * COLS].reshape(8, CZ, COLS)
            out_v[first : first + 8] = (tr_v[first : first + 8].astype(F32) + block).astype(BF16)
        pltpu.make_async_copy(out_v.at[rows_of_h(h)], out_hbm.at[rows_of_h(h)], st_sem.at[h]).start()

    for h in range(2):
        across(h).wait_send()
        for m in range(2):
            view = sbuf.at[m, pl.ds(0, DEV - 1), :, pl.ds(h * HALF, HALF), :]
            wait_all(view, ssem.at[m, h])
            wait_all(tsend.at[m, pl.ds(0, DEV - 1), pl.ds(h * HALF, HALF), :], tssem.at[m, h])
        pltpu.make_async_copy(out_v.at[rows_of_h(h)], out_hbm.at[rows_of_h(h)], st_sem.at[h]).wait()


def rows_of_h(h):
    return pl.ds(h * HALF, HALF)


def per_device(tp, trunk, coverage, chain_ids, chain_vec, wt, wp, wo, wf):
    vmem = pl.BlockSpec(memory_space=pltpu.VMEM)
    hbm = pl.BlockSpec(memory_space=pl.ANY)
    scratch = [
        pltpu.VMEM((ROWS, C, COLS), BF16),
        pltpu.VMEM((ROWS, CZ, COLS), BF16),
        pltpu.VMEM((ROWS, CZ, COLS), BF16),
        pltpu.VMEM((512, 512), BF16),
        pltpu.VMEM((512, 8 * CZ), BF16),
        pltpu.VMEM((2, 5, 512, 512), BF16),
        pltpu.VMEM((2, 512, 512), BF16),
        pltpu.VMEM((8 * CZ, 512), BF16),
        pltpu.VMEM((2, C, HALF, COLS), BF16),
        pltpu.VMEM((2, 512, 256), BF16),
        pltpu.VMEM((2, C, HALF, COLS), F32),
        pltpu.VMEM((2, DEV, 2, ROWS, COLS), BF16),
        pltpu.VMEM((2, DEV, 2, ROWS, COLS), BF16),
        pltpu.VMEM((2, DEV, ROWS, COLS), BF16),
        pltpu.VMEM((2, DEV, ROWS, COLS), BF16),
        pltpu.VMEM((2, C, HALF, COLS), BF16),
        pltpu.VMEM((2, C, HALF, COLS), BF16),
        pltpu.SemaphoreType.DMA((2,)),
        pltpu.SemaphoreType.DMA((2,)),
        pltpu.SemaphoreType.DMA((4, 2)),
        pltpu.SemaphoreType.DMA((2, 2)),
        pltpu.SemaphoreType.DMA((2, 2)),
        pltpu.SemaphoreType.DMA((2, 2)),
        pltpu.SemaphoreType.DMA((2, 2)),
        pltpu.SemaphoreType.DMA((2,)),
        pltpu.SemaphoreType.DMA((2,)),
    ]
    return pl.pallas_call(
        kernel,
        out_shape=jax.ShapeDtypeStruct(trunk.shape, BF16),
        in_specs=[hbm, hbm] + [vmem] * 7,
        out_specs=hbm,
        scratch_shapes=scratch,
        compiler_params=pltpu.CompilerParams(
            collective_id=0, has_side_effects=True, vmem_limit_bytes=60 * 1024 * 1024
        ),
        name="template_block",
    )(
        tp, trunk, coverage, chain_ids.reshape(1, 512), chain_vec.reshape(C, 1, 1),
        wt, wp, wo, wf,
    )


def solution(mesh):
    in_specs = (
        P("tmpl", "row", None, "col"), P("row", None, "col"),
        P(), P(), P(), P(), P(), P(), P(),
    )
    return jax.shard_map(
        per_device, mesh=mesh, in_specs=in_specs, out_specs=P("row", None, "col"), check_vma=False
    )
```

time: 300 us -> 68.3 us (0.23)
  waiting for transfers between devices: 158 us -> 0 us
  Pallas kernels: 0 us -> 63.7 us
  blocking collectives: 62.3 us -> 0 us
  matrix products: 34.3 us -> 0 us
  local copies, waits for them, and re-layouts: 20.8 us -> 4.39 us
  between operations: 13.7 us -> 0.01 us
  other arithmetic: 9.03 us -> 0 us
    reduce_scatter x1 -> x0, waiting for transfers between devices: 84.5 us -> none  [incoming(): lax.psum_scatter(jnp.einsum('kci,kcj->icj', left_rows, right_proj, prefer...]
    all_gather x1 -> x0, waiting for transfers between devices: 73.9 us -> none  [outgoing(): right_cols = lax.all_gather(right_proj, 'row', axis=0, tiled=True)]
    pallas_call x0 -> x1, Pallas kernels: none -> 63.7 us  [per_device(): pl.pallas_call(kernel, out_shape=jax.ShapeDtypeStruct(trunk.shape, BF16),...]
    all_to_all x3 -> x0, blocking collectives: 62.3 us -> none  [the longest x2 33.2 us: sent_to_all(): return lax.all_to_all(copies, axis, split_axis=0, concat_axis=0, tiled=True)]
    dot_general x8 -> x0, matrix products: 34.3 us -> none  [the longest x1 21.2 us: outgoing(): jnp.einsum('ick,jck->icj', left_proj, right_cols, preferred_element_type=...]
    convert_element_type x3 -> x0, local copies, waits for them, and re-layouts: 13.7 us -> none  [the longest x1 12 us: incoming(): return lax.psum_scatter(jnp.einsum('kci,kcj->icj', left_rows, right_proj,...]
    reduce_sum x11 -> x0, other arithmetic: 5.94 us -> none  [the longest x6 3.25 us: channel_norm(): spread = jnp.mean(centred * centred, axis=1, keepdims=True)]
  transfers between devices with their start and end apart: 2 -> 0, of which waited for: 2 -> 0; matrix products, arithmetic and copies ran while one was open for 0% -> 0% of each run, Pallas kernels for 0% -> 0%
where the time goes in v1:
time: 68.3 us; the launch traced here: 68.1 us
  Pallas kernels  63.7 us (93%)
  local copies, waits for them, and re-layouts  4.39 us (6%)
    pallas_call x1, Pallas kernels, per_device(): pl.pallas_call(kernel, out_shape=jax.ShapeDtypeStruct(trunk.shape, BF16),...  63.7 us
    unnamed x6, local copies, waits for them, and re-layouts  3.68 us

profile of v1, /device:TPU:1, one launch (start us, length us, event | category | flops | bytes accessed | tf_op | source)
XLA Modules:
  0.0 68.1 jit_solution(2067176104020300147)
XLA Ops:
  0.0 0.0 copy-start.1
  0.0 0.7 copy-done.1
  0.7 0.0 copy-start
  0.7 0.7 %copy.10.vec_ref = f32[64,1,1]{2,1,0:T(1,128)} copy(f32[64,1,1]{0,2,1:T(1,128)S(1)} %bitcast.3) | data formatting | bytes 512 | tf_op jit(solution)/shard_map/reshape | solution.py:348
  1.4 0.0 copy-done
  1.4 0.7 %copy.11.wf_ref = bf16[128,64]{1,0:T(8,128)(2,1)} copy(bf16[128,64]{0,1:T(8,128)(2,1)S(1)} %copy-done) | data formatting | bytes 32768 | tf_op args[8]
  2.1 63.7 %template_block.1 = bf16[32,128,128]{2,1,0:T(8,128)(2,1)} custom-call(bf16[1,32,64,128]{3,2,1,0:T(8,128)(2,1)} %tp_hbm.1, bf16[32,128,128]{2,1,0:T(8,128)(2,1)} %trunk_hbm.1, s32[2,512]{1,0:T(2,128)} %cover_ref.1, s32[1,512]{1,0:T(1,128)} %bitcast.2, f32[64,1,1]{2,1,0:T(1,128)} %copy.10.vec_ref, bf16[64,128]{1,0:T(8,128)(2,1)} %wt_ref.1, ...), custom_call_target="tpu_custom_call" | custom-call | tf_op jit(solution)/shard_map/template_block/pallas_call | solution.py:337
  65.8 2.3 %copy.13 = bf16[32,128,128]{2,1,0:T(8,128)(2,1)} copy(bf16[32,128,128]{2,1,0:T(8,128)(2,1)} %template_block.1) | data formatting | bytes 2097152
Async XLA Ops:
  0.0 0.7 copy-start.1
  0.7 0.7 %copy-start = (bf16[128,64]{0,1:T(8,128)(2,1)S(1)}, bf16[128,64]{0,1:T(8,128)(2,1)}, u32[]{:S(2)}) copy-start(bf16[128,64]{0,1:T(8,128)(2,1)} %param.17) | copy-start | bytes 49156

commit v2 on v1

v2 whole, which is shorter than its diff:
```python
import functools

import jax
import jax.numpy as jnp
from jax import lax
from jax.experimental import pallas as pl
from jax.experimental.pallas import tpu as pltpu
from jax.sharding import PartitionSpec as P

MESH = pl.DeviceIdType.MESH
EPS = 1e-05
F32 = jnp.float32
BF16 = jnp.bfloat16
ROWS, COLS, C, CZ = 32, 128, 64, 128
HALF = 16
DEV = 64


def dot(a, b):
    return jnp.dot(a, b, preferred_element_type=F32)


def iota(shape, dim):
    return lax.broadcasted_iota(jnp.int32, shape, dim)


def to_rhs(x):
    a = x[:, 0:8].reshape(512, COLS).astype(BF16)
    b = x[:, 8:16].reshape(512, COLS).astype(BF16)
    return jnp.concatenate([a, b], axis=1)


def from_out(o):
    a = o[:, 0:COLS].reshape(C, 8, COLS)
    b = o[:, COLS:].reshape(C, 8, COLS)
    return jnp.concatenate([a, b], axis=1)


def norm0(x):
    centred = x - jnp.mean(x, axis=0, keepdims=True)
    spread = jnp.mean(centred * centred, axis=0, keepdims=True)
    return centred * lax.rsqrt(spread + EPS)


def sigmoid(x):
    return 0.5 * jnp.tanh(0.5 * x) + 0.5


def kron_rows():
    return ((iota((512, C), 0) >> 3) == iota((512, C), 1)).astype(BF16)


def kron_cols():
    return ((iota((C, 512), 1) >> 3) == iota((C, 512), 0)).astype(BF16)


def kernel(
    tp_hbm, trunk_hbm, cover_ref, chain_ref, vec_ref, wt_ref, wp_ref, wo_ref, wf_ref,
    out_v,
    tp_v, tr_v, vec_v, diag_v, k_perm, k_trunk, k_proj, k_out, k_final,
    pair_v, normed_v, gate_v, tri_v, sbuf, rbuf, tsend, tbuf, psend, pbuf,
    ld_sem, own_sem, ssem, rsem, tssem, trsem, pssem, prsem,
):
    tmpl = lax.axis_index("tmpl")
    row = lax.axis_index("row")
    x = lax.axis_index("col")
    y, z = lax.div(row, 4), lax.rem(row, 4)
    me = x * 16 + row

    load_tp = pltpu.make_async_copy(tp_hbm.at[0], tp_v, ld_sem.at[0])
    load_tr = pltpu.make_async_copy(trunk_hbm, tr_v, ld_sem.at[1])
    load_tp.start()
    load_tr.start()

    peer_cols = [lax.rem(x + step, 4) for step in range(4)]

    def peer_row(step):
        mixed = lax.rem(step * 7, 16)
        return lax.rem(y + lax.div(mixed, 4), 4) * 4 + lax.rem(z + lax.rem(mixed, 4), 4)

    def each_peer(act):
        def rows_step(step, carry):
            prow = peer_row(step)
            for far in (2, 1, 3, 0):
                act(prow, peer_cols[far], peer_cols[far] * 16 + prow)
            return carry

        lax.fori_loop(1, 16, rows_step, 0)
        for far in (2, 1, 3):
            act(row, peer_cols[far], peer_cols[far] * 16 + row)

    barrier = pltpu.get_barrier_semaphore()

    def greet(prow, pcol, number):
        pl.semaphore_signal(
            barrier, inc=1, device_id=(tmpl, prow, pcol), device_id_type=MESH
        )

    each_peer(greet)
    pl.semaphore_signal(barrier, inc=1, device_id=(1 - tmpl, row, x), device_id_type=MESH)

    def send_all(source, target, send_sem, recv_sem, keep_sem):
        def send(prow, pcol, number):
            pltpu.make_async_remote_copy(
                src_ref=source(number), dst_ref=target, send_sem=send_sem, recv_sem=recv_sem,
                device_id=(tmpl, prow, pcol), device_id_type=MESH,
            ).start()

        each_peer(send)
        pltpu.make_async_copy(source(me), target, keep_sem).start()

    def wait_all(view, sem):
        pltpu.make_async_copy(view, view, sem).wait()

    def half(h):
        return pl.ds(h * HALF, HALF)

    def one_side(ref, number, side, h):
        return ref.at[0, number, side, half(h), :]

    def both_sides(ref, number, h):
        return ref.at[1, number, :, half(h), :]

    cover = cover_ref[...].astype(F32)
    picks = (iota((ROWS, 512), 1) == row * ROWS + iota((ROWS, 512), 0)).astype(BF16)

    def row_plane(line):
        spread = jnp.broadcast_to(line, (COLS, 512)).astype(BF16)
        return lax.dot_general(picks, spread, (((1,), (1,)), ((), ())), preferred_element_type=F32)

    lanes = pl.ds(pl.multiple_of(x * COLS, COLS), COLS)
    cols_of = cover_ref[:, lanes].astype(F32)
    masks = [row_plane(cover[t : t + 1]) * cols_of[t : t + 1] for t in range(2)]
    mask = jnp.where(tmpl == 0, masks[0], masks[1])
    count = jnp.maximum(masks[0] + masks[1], 1.0)
    chain_rows = row_plane(chain_ref[...].astype(F32))
    same_chain = jnp.where(chain_rows == chain_ref[:, lanes].astype(F32), 1.0, 0.0)

    for c in range(C):
        vec_v[c] = jnp.full((1, COLS), vec_ref[c], F32)
    tall_trunk = dot(kron_rows(), wt_ref[...])
    own_row = iota((512, CZ), 0) & 7
    for i in range(8):
        k_trunk[:, i * CZ : (i + 1) * CZ] = jnp.where(own_row == i, tall_trunk, 0.0).astype(BF16)
    left_row, left_col = iota((512, 512), 0), iota((512, 512), 1)
    k_perm[...] = jnp.where(
        (((left_row & 7) << 6) + (left_row >> 3)) == left_col, 1.0, 0.0
    ).astype(BF16)
    diag_v[...] = jnp.where((left_row & 7) == (left_col & 7), 1.0, 0.0)

    def kron8(w):
        tall = dot(kron_rows(), w).astype(BF16)
        return (dot(tall, kron_cols()) * diag_v[...]).astype(BF16)

    def product(m, side, h):
        rhs = normed_v[h]
        gate = from_out(dot(k_proj[m, 2 * side], rhs))
        value = from_out(dot(k_proj[m, 2 * side + 1], rhs))
        plane = mask[h * HALF : (h + 1) * HALF][None]
        sbuf[m, :, side, h * HALF : (h + 1) * HALF, :] = (plane * sigmoid(gate) * value).astype(BF16)

    def gates(m, h):
        gate_v[h] = sigmoid(from_out(dot(k_proj[m, 4], normed_v[h])))

    def updated(m, h, tri):
        tri_norm = to_rhs(norm0(tri))
        update = gate_v[h] * from_out(dot(k_out[m], tri_norm))
        return (pair_v[h].astype(F32) + update).astype(BF16)

    def send_side(side, h):
        send_all(
            lambda n: one_side(sbuf, n, side, h), one_side(rbuf, me, side, h),
            ssem.at[side, h], rsem.at[side, h], own_sem.at[side, h],
        )

    def wait_side(side, h):
        wait_all(rbuf.at[0, pl.ds(0, DEV - 1), side, half(h), :], rsem.at[side, h])
        pltpu.make_async_copy(
            one_side(sbuf, me, side, h), one_side(rbuf, me, side, h), own_sem.at[side, h]
        ).wait()

    load_tp.wait()
    load_tr.wait()
    for h in range(2):
        lo = h * HALF
        tr = tr_v[lo : lo + HALF].astype(F32)
        centred = tr - jnp.mean(tr, axis=1, keepdims=True)
        spread = jnp.mean(centred * centred, axis=1, keepdims=True)
        trn = (centred * lax.rsqrt(spread + EPS)).astype(BF16)
        rhs = jnp.concatenate(
            [trn[0:8].reshape(8 * CZ, COLS), trn[8:16].reshape(8 * CZ, COLS)], axis=1
        )
        pair = from_out(dot(k_trunk[...], rhs))
        tp = tp_v[lo : lo + HALF]
        rhs = jnp.concatenate([tp[0:8].reshape(512, COLS), tp[8:16].reshape(512, COLS)], axis=1)
        pair = pair + from_out(dot(k_perm[...], rhs))
        pair = pair + same_chain[lo : lo + HALF][None] * vec_v[...]
        pair = pair.astype(BF16)
        pair_v[h] = pair
        normed_v[h] = to_rhs(norm0(pair.astype(F32)))
        if h == 0:
            for d in (2, 3):
                k_proj[0, d] = kron8(wp_ref[0, d])
        product(0, 1, h)
        if h == 0:
            pl.semaphore_wait(barrier, DEV)
        send_side(1, h)
    for d in (0, 1):
        k_proj[0, d] = kron8(wp_ref[0, d])
    for h in range(2):
        product(0, 0, h)
        send_side(0, h)

    k_proj[0, 4] = kron8(wp_ref[0, 4])
    for h in range(2):
        gates(0, h)
    k_out[0] = kron8(wo_ref[0])
    for d in range(4):
        k_proj[1, d] = kron8(wp_ref[1, d])

    def send_tri(m, h):
        send_all(
            lambda n: tsend.at[m, n, half(h), :], tbuf.at[m, me, half(h), :],
            tssem.at[m, h], trsem.at[m, h], own_sem.at[3 + m, h],
        )

    def wait_tri(m, h):
        wait_all(tbuf.at[m, pl.ds(0, DEV - 1), half(h), :], trsem.at[m, h])
        pltpu.make_async_copy(
            tsend.at[m, me, half(h), :], tbuf.at[m, me, half(h), :], own_sem.at[3 + m, h]
        ).wait()
        return tbuf[m, :, h * HALF : (h + 1) * HALF, :].astype(F32)

    for h in range(2):
        wait_side(1, h)
    right = jnp.concatenate(
        [rbuf[0, q * 16 : (q + 1) * 16, 1].reshape(512, COLS) for q in range(4)], axis=1
    )
    for h in range(2):
        lo = h * HALF
        wait_side(0, h)
        left = jnp.concatenate(
            [rbuf[0, q * 16 : (q + 1) * 16, 0, lo : lo + HALF].reshape(256, COLS) for q in range(4)],
            axis=1,
        )
        tri = lax.dot_general(left, right, (((1,), (1,)), ((), ())), preferred_element_type=F32)
        for q in range(4):
            tsend[0, q * 16 : (q + 1) * 16, lo : lo + HALF, :] = (
                tri[:, q * COLS : (q + 1) * COLS].reshape(16, HALF, COLS).astype(BF16)
            )
        send_tri(0, h)
    for h in range(2):
        pair = updated(0, h, wait_tri(0, h))
        pair_v[h] = pair
        normed_v[h] = to_rhs(norm0(pair.astype(F32)))
        product(1, 0, h)
        product(1, 1, h)
        send_all(
            lambda n: both_sides(sbuf, n, h), both_sides(rbuf, me, h),
            ssem.at[2, h], rsem.at[2, h], own_sem.at[2, h],
        )
    k_proj[1, 4] = kron8(wp_ref[1, 4])
    for h in range(2):
        gates(1, h)
    k_out[1] = kron8(wo_ref[1])
    wide = lax.dot_general(wf_ref[...], kron_cols(), (((0,), (0,)), ((), ())), preferred_element_type=F32)
    own_col = iota((CZ, 512), 1) & 7
    for i in range(8):
        k_final[i * CZ : (i + 1) * CZ, :] = jnp.where(own_col == i, wide, 0.0).astype(BF16)

    for h in range(2):
        wait_all(rbuf.at[1, pl.ds(0, DEV - 1), :, half(h), :], rsem.at[2, h])
        pltpu.make_async_copy(both_sides(sbuf, me, h), both_sides(rbuf, me, h), own_sem.at[2, h]).wait()
        left, right = [
            jnp.concatenate(
                [
                    rbuf[1, q * 16 : (q + 1) * 16, side, h * HALF : (h + 1) * HALF].reshape(256, COLS)
                    for q in range(4)
                ],
                axis=1,
            )
            for side in range(2)
        ]
        tri = lax.dot_general(left, right, (((0,), (0,)), ((), ())), preferred_element_type=F32)
        if h == 0:
            tri_v[...] = tri
        else:
            tri = tri + tri_v[...]
    for q in range(4):
        tsend[1, q * 16 : (q + 1) * 16, :, :] = (
            tri[:, q * COLS : (q + 1) * COLS].reshape(16, ROWS, COLS).astype(BF16)
        )
    for h in range(2):
        send_tri(1, h)

    def across(h):
        return pltpu.make_async_remote_copy(
            src_ref=psend.at[h], dst_ref=pbuf.at[h], send_sem=pssem.at[h], recv_sem=prsem.at[h],
            device_id=(1 - tmpl, row, x), device_id_type=MESH,
        )

    for h in range(2):
        pair = updated(1, h, wait_tri(1, h))
        pooled = mask[h * HALF : (h + 1) * HALF][None] * norm0(pair.astype(F32))
        psend[h] = pooled.astype(BF16)
        across(h).start()
    for h in range(2):
        lo = h * HALF
        across(h).wait_recv()
        pooled = psend[h].astype(F32) + pbuf[h].astype(F32)
        hidden = jnp.maximum(pooled / count[lo : lo + HALF][None], 0.0)
        out = dot(k_final[...], to_rhs(hidden))
        for side in range(2):
            first = lo + 8 * side
            block = out[:, side * COLS : (side + 1) * COLS].reshape(8, CZ, COLS)
            out_v[first : first + 8] = (tr_v[first : first + 8].astype(F32) + block).astype(BF16)

    for h in range(2):
        across(h).wait_send()
        for side in range(2):
            wait_all(sbuf.at[0, pl.ds(0, DEV - 1), side, half(h), :], ssem.at[side, h])
        wait_all(sbuf.at[1, pl.ds(0, DEV - 1), :, half(h), :], ssem.at[2, h])
        for m in range(2):
            wait_all(tsend.at[m, pl.ds(0, DEV - 1), half(h), :], tssem.at[m, h])


def per_device(tp, trunk, coverage, chain_ids, chain_vec, wt, wp, wo, wf):
    vmem = pl.BlockSpec(memory_space=pltpu.VMEM)
    hbm = pl.BlockSpec(memory_space=pl.ANY)
    scratch = [
        pltpu.VMEM((ROWS, C, COLS), BF16),
        pltpu.VMEM((ROWS, CZ, COLS), BF16),
        pltpu.VMEM((C, 1, COLS), F32),
        pltpu.VMEM((512, 512), F32),
        pltpu.VMEM((512, 512), BF16),
        pltpu.VMEM((512, 8 * CZ), BF16),
        pltpu.VMEM((2, 5, 512, 512), BF16),
        pltpu.VMEM((2, 512, 512), BF16),
        pltpu.VMEM((8 * CZ, 512), BF16),
        pltpu.VMEM((2, C, HALF, COLS), BF16),
        pltpu.VMEM((2, 512, 256), BF16),
        pltpu.VMEM((2, C, HALF, COLS), F32),
        pltpu.VMEM((512, 512), F32),
        pltpu.VMEM((2, DEV, 2, ROWS, COLS), BF16),
        pltpu.VMEM((2, DEV, 2, ROWS, COLS), BF16),
        pltpu.VMEM((2, DEV, ROWS, COLS), BF16),
        pltpu.VMEM((2, DEV, ROWS, COLS), BF16),
        pltpu.VMEM((2, C, HALF, COLS), BF16),
        pltpu.VMEM((2, C, HALF, COLS), BF16),
        pltpu.SemaphoreType.DMA((2,)),
        pltpu.SemaphoreType.DMA((5, 2)),
        pltpu.SemaphoreType.DMA((3, 2)),
        pltpu.SemaphoreType.DMA((3, 2)),
        pltpu.SemaphoreType.DMA((2, 2)),
        pltpu.SemaphoreType.DMA((2, 2)),
        pltpu.SemaphoreType.DMA((2,)),
        pltpu.SemaphoreType.DMA((2,)),
    ]
    return pl.pallas_call(
        kernel,
        out_shape=pltpu.VMEM(trunk.shape, BF16),
        in_specs=[hbm, hbm, vmem, vmem, pl.BlockSpec(memory_space=pltpu.SMEM)] + [vmem] * 4,
        out_specs=vmem,
        scratch_shapes=scratch,
        compiler_params=pltpu.CompilerParams(
            collective_id=0, has_side_effects=True, vmem_limit_bytes=60 * 1024 * 1024
        ),
        name="template_block",
    )(
        tp, trunk, coverage, chain_ids.reshape(1, 512), chain_vec, wt, wp, wo, wf.T,
    )


def solution(mesh):
    in_specs = (
        P("tmpl", "row", None, "col"), P("row", None, "col"),
        P(), P(), P(), P(), P(), P(), P(),
    )
    return jax.shard_map(
        per_device, mesh=mesh, in_specs=in_specs, out_specs=P("row", None, "col"), check_vma=False
    )
```

time: 68.3 us -> 60.7 us (0.89)
  Pallas kernels: 63.7 us -> 59.6 us
  local copies, waits for them, and re-layouts: 4.39 us -> 0.97 us
    pallas_call x1, Pallas kernels: 63.7 us -> 59.6 us  [per_device(): pl.pallas_call(kernel, out_shape=pltpu.VMEM(trunk.shape, BF16), in_specs=...]
    unnamed x6 -> x1, local copies, waits for them, and re-layouts: 3.68 us -> 0.97 us
    reshape x1 -> x0, local copies, waits for them, and re-layouts: 0.71 us -> none  [per_device(): chain_vec.reshape(C, 1, 1)]
where the time goes in v2:
time: 60.7 us; the launch traced here: 60.6 us
  Pallas kernels  59.6 us (98%)
  local copies, waits for them, and re-layouts  0.97 us (2%)
    pallas_call x1, Pallas kernels, per_device(): pl.pallas_call(kernel, out_shape=pltpu.VMEM(trunk.shape, BF16), in_specs=...  59.6 us

profile of v2, /device:TPU:1, one launch (start us, length us, event | category | flops | bytes accessed | tf_op | source)
XLA Modules:
  0.0 60.6 jit_solution(1102982920701005871)
XLA Ops:
  0.0 59.6 %template_block.1 = bf16[32,128,128]{2,1,0:T(8,128)(2,1)S(1)} custom-call(bf16[1,32,64,128]{3,2,1,0:T(8,128)(2,1)} %tp_hbm.1, bf16[32,128,128]{2,1,0:T(8,128)(2,1)} %trunk_hbm.1, s32[2,512]{1,0:T(2,128)} %cover_ref.1, s32[1,512]{1,0:T(1,128)} %bitcast.3, f32[64]{0:T(128)} %vec_ref.1, bf16[64,128]{1,0:T(8,128)(2,1)} %wt_ref.1, bf16[2,5,64,64]{3,2,1,0:T(8,128)(2,1)} %wp_ref.1, ...), custom_call_target="tpu_custom_call" | custom-call | tf_op jit(solution)/shard_map/template_block/pallas_call | solution.py:359
  59.6 1.0 %copy.11 = bf16[32,128,128]{2,1,0:T(8,128)(2,1)} copy(bf16[32,128,128]{2,1,0:T(8,128)(2,1)S(1)} %template_block.1) | data formatting | bytes 2097152

commit v3 on v2

--- a/solution.py
+++ b/solution.py
@@ -55,9 +55,9 @@
 
 
 def kernel(
-    tp_hbm, trunk_hbm, cover_ref, chain_ref, vec_ref, wt_ref, wp_ref, wo_ref, wf_ref,
+    tp_hbm, trunk_hbm, cover_hbm, chain_hbm, vec_hbm, wt_hbm, wp_hbm, wo_hbm, wf_hbm,
     out_v,
-    tp_v, tr_v, vec_v, diag_v, k_perm, k_trunk, k_proj, k_out, k_final,
+    cover_ref, chain_ref, vec_ref, wt_ref, wp_ref, wo_ref, wf_ref, tp_v, tr_v, vec_v, diag_v, k_perm, k_trunk, k_proj, k_out, k_final,
     pair_v, normed_v, gate_v, tri_v, sbuf, rbuf, tsend, tbuf, psend, pbuf,
     ld_sem, own_sem, ssem, rsem, tssem, trsem, pssem, prsem,
 ):
@@ -67,25 +67,26 @@
     y, z = lax.div(row, 4), lax.rem(row, 4)
     me = x * 16 + row
 
-    load_tp = pltpu.make_async_copy(tp_hbm.at[0], tp_v, ld_sem.at[0])
-    load_tr = pltpu.make_async_copy(trunk_hbm, tr_v, ld_sem.at[1])
-    load_tp.start()
-    load_tr.start()
+    def load(number, source, target):
+        copy = pltpu.make_async_copy(source, target, ld_sem.at[number])
+        copy.start()
+        return copy
 
     peer_cols = [lax.rem(x + step, 4) for step in range(4)]
 
-    def peer_row(step):
-        mixed = lax.rem(step * 7, 16)
-        return lax.rem(y + lax.div(mixed, 4), 4) * 4 + lax.rem(z + lax.rem(mixed, 4), 4)
+    def away(step):
+        return 2 - step + 3 * lax.div(step, 2) - 2 * lax.div(step + 1, 4)
 
     def each_peer(act):
         def rows_step(step, carry):
-            prow = peer_row(step)
+            py = lax.rem(y + away(lax.div(step, 4)), 4)
+            pz = lax.rem(z + away(lax.rem(step, 4)), 4)
+            prow = py * 4 + pz
             for far in (2, 1, 3, 0):
                 act(prow, peer_cols[far], peer_cols[far] * 16 + prow)
             return carry
 
-        lax.fori_loop(1, 16, rows_step, 0)
+        lax.fori_loop(0, 15, rows_step, 0)
         for far in (2, 1, 3):
             act(row, peer_cols[far], peer_cols[far] * 16 + row)
 
@@ -98,6 +99,17 @@
 
     each_peer(greet)
     pl.semaphore_signal(barrier, inc=1, device_id=(1 - tmpl, row, x), device_id_type=MESH)
+
+    tops = pl.ds(0, HALF), pl.ds(HALF, HALF)
+    small = [
+        load(0, cover_hbm, cover_ref), load(1, chain_hbm, chain_ref),
+        load(2, vec_hbm, vec_ref), load(3, wt_hbm, wt_ref), load(4, wp_hbm, wp_ref),
+    ]
+    load_tr, load_tp = [], []
+    for h in range(2):
+        load_tr.append(load(5 + h, trunk_hbm.at[tops[h]], tr_v.at[tops[h]]))
+        load_tp.append(load(7 + h, tp_hbm.at[0, tops[h]], tp_v.at[tops[h]]))
+    late = [load(9, wo_hbm, wo_ref), load(10, wf_hbm, wf_ref)]
 
     def send_all(source, target, send_sem, recv_sem, keep_sem):
         def send(prow, pcol, number):
@@ -115,11 +127,16 @@
     def half(h):
         return pl.ds(h * HALF, HALF)
 
-    def one_side(ref, number, side, h):
-        return ref.at[0, number, side, half(h), :]
-
-    def both_sides(ref, number, h):
-        return ref.at[1, number, :, half(h), :]
+    def block(ref, m, number, side, h):
+        return ref.at[m, number, side, half(h), :]
+
+    left_row, left_col = iota((512, 512), 0), iota((512, 512), 1)
+    k_perm[...] = jnp.where(
+        (((left_row & 7) << 6) + (left_row >> 3)) == left_col, 1.0, 0.0
+    ).astype(BF16)
+    diag_v[...] = jnp.where((left_row & 7) == (left_col & 7), 1.0, 0.0)
+    for copy in small:
+        copy.wait()
 
     cover = cover_ref[...].astype(F32)
     picks = (iota((ROWS, 512), 1) == row * ROWS + iota((ROWS, 512), 0)).astype(BF16)
@@ -142,12 +159,6 @@
     own_row = iota((512, CZ), 0) & 7
     for i in range(8):
         k_trunk[:, i * CZ : (i + 1) * CZ] = jnp.where(own_row == i, tall_trunk, 0.0).astype(BF16)
-    left_row, left_col = iota((512, 512), 0), iota((512, 512), 1)
-    k_perm[...] = jnp.where(
-        (((left_row & 7) << 6) + (left_row >> 3)) == left_col, 1.0, 0.0
-    ).astype(BF16)
-    diag_v[...] = jnp.where((left_row & 7) == (left_col & 7), 1.0, 0.0)
-
     def kron8(w):
         tall = dot(kron_rows(), w).astype(BF16)
         return (dot(tall, kron_cols()) * diag_v[...]).astype(BF16)
@@ -167,22 +178,24 @@
         update = gate_v[h] * from_out(dot(k_out[m], tri_norm))
         return (pair_v[h].astype(F32) + update).astype(BF16)
 
-    def send_side(side, h):
+    def send_side(m, side, h):
         send_all(
-            lambda n: one_side(sbuf, n, side, h), one_side(rbuf, me, side, h),
-            ssem.at[side, h], rsem.at[side, h], own_sem.at[side, h],
-        )
-
-    def wait_side(side, h):
-        wait_all(rbuf.at[0, pl.ds(0, DEV - 1), side, half(h), :], rsem.at[side, h])
+            lambda n: block(sbuf, m, n, side, h), block(rbuf, m, me, side, h),
+            ssem.at[m, side, h], rsem.at[m, side, h], own_sem.at[m, side, h],
+        )
+
+    def wait_side(m, side, h):
+        wait_all(rbuf.at[m, pl.ds(0, DEV - 1), side, half(h), :], rsem.at[m, side, h])
         pltpu.make_async_copy(
-            one_side(sbuf, me, side, h), one_side(rbuf, me, side, h), own_sem.at[side, h]
+            block(sbuf, m, me, side, h), block(rbuf, m, me, side, h), own_sem.at[m, side, h]
         ).wait()
 
-    load_tp.wait()
-    load_tr.wait()
+    for d in (2, 3):
+        k_proj[0, d] = kron8(wp_ref[0, d])
     for h in range(2):
         lo = h * HALF
+        load_tr[h].wait()
+        load_tp[h].wait()
         tr = tr_v[lo : lo + HALF].astype(F32)
         centred = tr - jnp.mean(tr, axis=1, keepdims=True)
         spread = jnp.mean(centred * centred, axis=1, keepdims=True)
@@ -198,22 +211,22 @@
         pair = pair.astype(BF16)
         pair_v[h] = pair
         normed_v[h] = to_rhs(norm0(pair.astype(F32)))
-        if h == 0:
-            for d in (2, 3):
-                k_proj[0, d] = kron8(wp_ref[0, d])
         product(0, 1, h)
         if h == 0:
             pl.semaphore_wait(barrier, DEV)
-        send_side(1, h)
+        send_side(0, 1, h)
     for d in (0, 1):
         k_proj[0, d] = kron8(wp_ref[0, d])
     for h in range(2):
         product(0, 0, h)
-        send_side(0, h)
+        send_side(0, 0, h)
+
 
     k_proj[0, 4] = kron8(wp_ref[0, 4])
     for h in range(2):
         gates(0, h)
+    for copy in late:
+        copy.wait()
     k_out[0] = kron8(wo_ref[0])
     for d in range(4):
         k_proj[1, d] = kron8(wp_ref[1, d])
@@ -221,24 +234,24 @@
     def send_tri(m, h):
         send_all(
             lambda n: tsend.at[m, n, half(h), :], tbuf.at[m, me, half(h), :],
-            tssem.at[m, h], trsem.at[m, h], own_sem.at[3 + m, h],
+            tssem.at[m, h], trsem.at[m, h], own_sem.at[2, m, h],
         )
 
     def wait_tri(m, h):
         wait_all(tbuf.at[m, pl.ds(0, DEV - 1), half(h), :], trsem.at[m, h])
         pltpu.make_async_copy(
-            tsend.at[m, me, half(h), :], tbuf.at[m, me, half(h), :], own_sem.at[3 + m, h]
+            tsend.at[m, me, half(h), :], tbuf.at[m, me, half(h), :], own_sem.at[2, m, h]
         ).wait()
         return tbuf[m, :, h * HALF : (h + 1) * HALF, :].astype(F32)
 
     for h in range(2):
-        wait_side(1, h)
+        wait_side(0, 1, h)
     right = jnp.concatenate(
         [rbuf[0, q * 16 : (q + 1) * 16, 1].reshape(512, COLS) for q in range(4)], axis=1
     )
     for h in range(2):
         lo = h * HALF
-        wait_side(0, h)
+        wait_side(0, 0, h)
         left = jnp.concatenate(
             [rbuf[0, q * 16 : (q + 1) * 16, 0, lo : lo + HALF].reshape(256, COLS) for q in range(4)],
             axis=1,
@@ -253,12 +266,9 @@
         pair = updated(0, h, wait_tri(0, h))
         pair_v[h] = pair
         normed_v[h] = to_rhs(norm0(pair.astype(F32)))
-        product(1, 0, h)
-        product(1, 1, h)
-        send_all(
-            lambda n: both_sides(sbuf, n, h), both_sides(rbuf, me, h),
-            ssem.at[2, h], rsem.at[2, h], own_sem.at[2, h],
-        )
+        for side in (1, 0):
+            product(1, side, h)
+            send_side(1, side, h)
     k_proj[1, 4] = kron8(wp_ref[1, 4])
     for h in range(2):
         gates(1, h)
@@ -269,8 +279,8 @@
         k_final[i * CZ : (i + 1) * CZ, :] = jnp.where(own_col == i, wide, 0.0).astype(BF16)
 
     for h in range(2):
-        wait_all(rbuf.at[1, pl.ds(0, DEV - 1), :, half(h), :], rsem.at[2, h])
-        pltpu.make_async_copy(both_sides(sbuf, me, h), both_sides(rbuf, me, h), own_sem.at[2, h]).wait()
+        for side in (1, 0):
+            wait_side(1, side, h)
         left, right = [
             jnp.concatenate(
                 [
@@ -304,23 +314,21 @@
         pooled = mask[h * HALF : (h + 1) * HALF][None] * norm0(pair.astype(F32))
         psend[h] = pooled.astype(BF16)
         across(h).start()
-    for h in range(2):
+        across(h).wait_recv()
         lo = h * HALF
-        across(h).wait_recv()
-        pooled = psend[h].astype(F32) + pbuf[h].astype(F32)
-        hidden = jnp.maximum(pooled / count[lo : lo + HALF][None], 0.0)
+        total = psend[h].astype(F32) + pbuf[h].astype(F32)
+        hidden = jnp.maximum(total / count[lo : lo + HALF][None], 0.0)
         out = dot(k_final[...], to_rhs(hidden))
         for side in range(2):
             first = lo + 8 * side
-            block = out[:, side * COLS : (side + 1) * COLS].reshape(8, CZ, COLS)
-            out_v[first : first + 8] = (tr_v[first : first + 8].astype(F32) + block).astype(BF16)
+            added = out[:, side * COLS : (side + 1) * COLS].reshape(8, CZ, COLS)
+            out_v[first : first + 8] = (tr_v[first : first + 8].astype(F32) + added).astype(BF16)
 
     for h in range(2):
         across(h).wait_send()
-        for side in range(2):
-            wait_all(sbuf.at[0, pl.ds(0, DEV - 1), side, half(h), :], ssem.at[side, h])
-        wait_all(sbuf.at[1, pl.ds(0, DEV - 1), :, half(h), :], ssem.at[2, h])
         for m in range(2):
+            for side in range(2):
+                wait_all(sbuf.at[m, pl.ds(0, DEV - 1), side, half(h), :], ssem.at[m, side, h])
             wait_all(tsend.at[m, pl.ds(0, DEV - 1), half(h), :], tssem.at[m, h])
 
 
@@ -328,6 +336,13 @@
     vmem = pl.BlockSpec(memory_space=pltpu.VMEM)
     hbm = pl.BlockSpec(memory_space=pl.ANY)
     scratch = [
+        pltpu.VMEM((2, 512), jnp.int32),
+        pltpu.VMEM((1, 512), jnp.int32),
+        pltpu.SMEM((C,), F32),
+        pltpu.VMEM((C, CZ), BF16),
+        pltpu.VMEM((2, 5, C, C), BF16),
+        pltpu.VMEM((2, C, C), BF16),
+        pltpu.VMEM((C, CZ), BF16),
         pltpu.VMEM((ROWS, C, COLS), BF16),
         pltpu.VMEM((ROWS, CZ, COLS), BF16),
         pltpu.VMEM((C, 1, COLS), F32),
@@ -347,10 +362,10 @@
         pltpu.VMEM((2, DEV, ROWS, COLS), BF16),
         pltpu.VMEM((2, C, HALF, COLS), BF16),
         pltpu.VMEM((2, C, HALF, COLS), BF16),
-        pltpu.SemaphoreType.DMA((2,)),
-        pltpu.SemaphoreType.DMA((5, 2)),
-        pltpu.SemaphoreType.DMA((3, 2)),
-        pltpu.SemaphoreType.DMA((3, 2)),
+        pltpu.SemaphoreType.DMA((11,)),
+        pltpu.SemaphoreType.DMA((3, 2, 2)),
+        pltpu.SemaphoreType.DMA((2, 2, 2)),
+        pltpu.SemaphoreType.DMA((2, 2, 2)),
         pltpu.SemaphoreType.DMA((2, 2)),
         pltpu.SemaphoreType.DMA((2, 2)),
         pltpu.SemaphoreType.DMA((2,)),
@@ -359,7 +374,7 @@
     return pl.pallas_call(
         kernel,
         out_shape=pltpu.VMEM(trunk.shape, BF16),
-        in_specs=[hbm, hbm, vmem, vmem, pl.BlockSpec(memory_space=pltpu.SMEM)] + [vmem] * 4,
+        in_specs=[hbm] * 9,
         out_specs=vmem,
         scratch_shapes=scratch,
         compiler_params=pltpu.CompilerParams(

time: 60.7 us -> 59.9 us (0.987)
  Pallas kernels: 59.6 us -> 58.8 us
    pallas_call x1, Pallas kernels: 59.6 us -> 58.8 us  [per_device(): pl.pallas_call(kernel, out_shape=pltpu.VMEM(trunk.shape, BF16), in_specs=...]
where the time goes in v3:
time: 59.9 us; the launch traced here: 59.8 us
  Pallas kernels  58.8 us (98%)
  local copies, waits for them, and re-layouts  0.97 us (2%)
    pallas_call x1, Pallas kernels, per_device(): pl.pallas_call(kernel, out_shape=pltpu.VMEM(trunk.shape, BF16), in_specs=...  58.8 us

profile of v3, /device:TPU:1, one launch (start us, length us, event | category | flops | bytes accessed | tf_op | source)
XLA Modules:
  0.0 59.8 jit_solution(18099662737358598036)
XLA Ops:
  0.0 58.8 %template_block.1 = bf16[32,128,128]{2,1,0:T(8,128)(2,1)S(1)} custom-call(bf16[1,32,64,128]{3,2,1,0:T(8,128)(2,1)} %tp_hbm.1, bf16[32,128,128]{2,1,0:T(8,128)(2,1)} %trunk_hbm.1, s32[2,512]{1,0:T(2,128)} %cover_hbm.1, s32[1,512]{1,0:T(1,128)} %bitcast.3, f32[64]{0:T(128)} %vec_hbm.1, bf16[64,128]{1,0:T(8,128)(2,1)} %wt_hbm.1, bf16[2,5,64,64]{3,2,1,0:T(8,128)(2,1)} %wp_hbm.1, ...), custom_call_target="tpu_custom_call" | custom-call | tf_op jit(solution)/shard_map/template_block/pallas_call | solution.py:374
  58.9 1.0 %copy.11 = bf16[32,128,128]{2,1,0:T(8,128)(2,1)} copy(bf16[32,128,128]{2,1,0:T(8,128)(2,1)S(1)} %template_block.1) | data formatting | bytes 2097152

commit v4 on v3

--- a/solution.py
+++ b/solution.py
@@ -57,8 +57,8 @@
 def kernel(
     tp_hbm, trunk_hbm, cover_hbm, chain_hbm, vec_hbm, wt_hbm, wp_hbm, wo_hbm, wf_hbm,
     out_v,
-    cover_ref, chain_ref, vec_ref, wt_ref, wp_ref, wo_ref, wf_ref, tp_v, tr_v, vec_v, diag_v, k_perm, k_trunk, k_proj, k_out, k_final,
-    pair_v, normed_v, gate_v, tri_v, sbuf, rbuf, tsend, tbuf, psend, pbuf,
+    cover_ref, chain_ref, vec_ref, wt_ref, wp_ref, wo_ref, wf_ref, tp_v, tr_v, vec_v, diag_v, k_perm, k_trunk, k_proj, k_out, k_final, k_lane,
+    pair_v, normed_v, gate_v, sbuf, rbuf, tsend, tbuf, psend, pbuf,
     ld_sem, own_sem, ssem, rsem, tssem, trsem, pssem, prsem,
 ):
     tmpl = lax.axis_index("tmpl")
@@ -169,6 +169,17 @@
         value = from_out(dot(k_proj[m, 2 * side + 1], rhs))
         plane = mask[h * HALF : (h + 1) * HALF][None]
         sbuf[m, :, side, h * HALF : (h + 1) * HALF, :] = (plane * sigmoid(gate) * value).astype(BF16)
+
+    def left_by_parts(h):
+        rhs = dot(normed_v[h], k_lane[h]).astype(BF16)
+        gate = from_out(dot(k_proj[1, 0], rhs))
+        value = from_out(dot(k_proj[1, 1], rhs))
+        plane = dot(mask[h * HALF : (h + 1) * HALF].astype(BF16), k_lane[h, 0:COLS, 0:COLS])[None]
+        left = (plane * sigmoid(gate) * value).astype(BF16)
+        for lanes_of in range(2):
+            first = (h ^ lanes_of) * HALF
+            cut = slice(lanes_of * 64, lanes_of * 64 + 64)
+            sbuf[1, :, 0, first : first + HALF, cut] = left[:, :, cut]
 
     def gates(m, h):
         gate_v[h] = sigmoid(from_out(dot(k_proj[m, 4], normed_v[h])))
@@ -230,6 +241,11 @@
     k_out[0] = kron8(wo_ref[0])
     for d in range(4):
         k_proj[1, d] = kron8(wp_ref[1, d])
+    old, new = iota((256, 256), 0), iota((256, 256), 1)
+    for h in range(2):
+        half_of = ((new >> 6) & 1) ^ h
+        place = (new & 15) + (((new >> 4) & 3) << 5) + (half_of << 4) + (new & COLS)
+        k_lane[h] = jnp.where(old == place, 1.0, 0.0).astype(BF16)
 
     def send_tri(m, h):
         send_all(
@@ -266,9 +282,11 @@
         pair = updated(0, h, wait_tri(0, h))
         pair_v[h] = pair
         normed_v[h] = to_rhs(norm0(pair.astype(F32)))
-        for side in (1, 0):
-            product(1, side, h)
-            send_side(1, side, h)
+        product(1, 1, h)
+        send_side(1, 1, h)
+        left_by_parts(h)
+    for part in range(2):
+        send_side(1, 0, part)
     k_proj[1, 4] = kron8(wp_ref[1, 4])
     for h in range(2):
         gates(1, h)
@@ -278,30 +296,32 @@
     for i in range(8):
         k_final[i * CZ : (i + 1) * CZ, :] = jnp.where(own_col == i, wide, 0.0).astype(BF16)
 
-    for h in range(2):
-        for side in (1, 0):
-            wait_side(1, side, h)
-        left, right = [
-            jnp.concatenate(
-                [
-                    rbuf[1, q * 16 : (q + 1) * 16, side, h * HALF : (h + 1) * HALF].reshape(256, COLS)
-                    for q in range(4)
-                ],
-                axis=1,
+    def stacked(side, h):
+        return jnp.concatenate(
+            [
+                rbuf[1, q * 16 : (q + 1) * 16, side, h * HALF : (h + 1) * HALF].reshape(256, COLS)
+                for q in range(4)
+            ],
+            axis=1,
+        )
+
+    for h in range(2):
+        wait_side(1, 1, h)
+    rights = [stacked(1, h) for h in range(2)]
+    for part in range(2):
+        wait_side(1, 0, part)
+        left = stacked(0, part)
+        sums = [
+            lax.dot_general(left, rights[h], (((0,), (0,)), ((), ())), preferred_element_type=F32)
+            .reshape(4, COLS, 512)
+            for h in (part, 1 - part)
+        ]
+        tri = (sums[0][:, 0:64] + sums[1][:, 64:COLS]).reshape(16, HALF, 512)
+        for q in range(4):
+            tsend[1, q * 16 : (q + 1) * 16, part * HALF : (part + 1) * HALF, :] = (
+                tri[:, :, q * COLS : (q + 1) * COLS].astype(BF16)
             )
-            for side in range(2)
-        ]
-        tri = lax.dot_general(left, right, (((0,), (0,)), ((), ())), preferred_element_type=F32)
-        if h == 0:
-            tri_v[...] = tri
-        else:
-            tri = tri + tri_v[...]
-    for q in range(4):
-        tsend[1, q * 16 : (q + 1) * 16, :, :] = (
-            tri[:, q * COLS : (q + 1) * COLS].reshape(16, ROWS, COLS).astype(BF16)
-        )
-    for h in range(2):
-        send_tri(1, h)
+        send_tri(1, part)
 
     def across(h):
         return pltpu.make_async_remote_copy(
@@ -314,6 +334,7 @@
         pooled = mask[h * HALF : (h + 1) * HALF][None] * norm0(pair.astype(F32))
         psend[h] = pooled.astype(BF16)
         across(h).start()
+    for h in range(2):
         across(h).wait_recv()
         lo = h * HALF
         total = psend[h].astype(F32) + pbuf[h].astype(F32)
@@ -352,10 +373,10 @@
         pltpu.VMEM((2, 5, 512, 512), BF16),
         pltpu.VMEM((2, 512, 512), BF16),
         pltpu.VMEM((8 * CZ, 512), BF16),
+        pltpu.VMEM((2, 256, 256), BF16),
         pltpu.VMEM((2, C, HALF, COLS), BF16),
         pltpu.VMEM((2, 512, 256), BF16),
         pltpu.VMEM((2, C, HALF, COLS), F32),
-        pltpu.VMEM((512, 512), F32),
         pltpu.VMEM((2, DEV, 2, ROWS, COLS), BF16),
         pltpu.VMEM((2, DEV, 2, ROWS, COLS), BF16),
         pltpu.VMEM((2, DEV, ROWS, COLS), BF16),

time: 59.9 us -> 58.7 us (0.980)
  Pallas kernels: 58.8 us -> 57.7 us
    pallas_call x1, Pallas kernels: 58.8 us -> 57.7 us  [per_device(): pl.pallas_call(kernel, out_shape=pltpu.VMEM(trunk.shape, BF16), in_specs=...]
where the time goes in v4:
time: 58.7 us; the launch traced here: 58.6 us
  Pallas kernels  57.7 us (98%)
  local copies, waits for them, and re-layouts  0.97 us (2%)
    pallas_call x1, Pallas kernels, per_device(): pl.pallas_call(kernel, out_shape=pltpu.VMEM(trunk.shape, BF16), in_specs=...  57.7 us

profile of v4, /device:TPU:1, one launch (start us, length us, event | category | flops | bytes accessed | tf_op | source)
XLA Modules:
  0.0 58.6 jit_solution(2633519799449075857)
XLA Ops:
  0.0 57.7 %template_block.1 = bf16[32,128,128]{2,1,0:T(8,128)(2,1)S(1)} custom-call(bf16[1,32,64,128]{3,2,1,0:T(8,128)(2,1)} %tp_hbm.1, bf16[32,128,128]{2,1,0:T(8,128)(2,1)} %trunk_hbm.1, s32[2,512]{1,0:T(2,128)} %cover_hbm.1, s32[1,512]{1,0:T(1,128)} %bitcast.3, f32[64]{0:T(128)} %vec_hbm.1, bf16[64,128]{1,0:T(8,128)(2,1)} %wt_hbm.1, bf16[2,5,64,64]{3,2,1,0:T(8,128)(2,1)} %wp_hbm.1, ...), custom_call_target="tpu_custom_call" | custom-call | tf_op jit(solution)/shard_map/template_block/pallas_call | solution.py:395
  57.7 1.0 %copy.11 = bf16[32,128,128]{2,1,0:T(8,128)(2,1)} copy(bf16[32,128,128]{2,1,0:T(8,128)(2,1)S(1)} %template_block.1) | data formatting | bytes 2097152

commit v5 on v4

--- a/solution.py
+++ b/solution.py
@@ -14,6 +14,11 @@
 ROWS, COLS, C, CZ = 32, 128, 64, 128
 HALF = 16
 DEV = 64
+STEPS = (2, 1, 3, 0)
+FAR_FIRST = sorted(
+    [(dx, dy, dz) for dy in STEPS for dz in STEPS for dx in STEPS if dx or dy or dz],
+    key=lambda step: -sum(min(part, 4 - part) for part in step),
+)
 
 
 def dot(a, b):
@@ -73,22 +78,13 @@
         return copy
 
     peer_cols = [lax.rem(x + step, 4) for step in range(4)]
-
-    def away(step):
-        return 2 - step + 3 * lax.div(step, 2) - 2 * lax.div(step + 1, 4)
+    peer_ys = [lax.rem(y + step, 4) * 4 for step in range(4)]
+    peer_zs = [lax.rem(z + step, 4) for step in range(4)]
 
     def each_peer(act):
-        def rows_step(step, carry):
-            py = lax.rem(y + away(lax.div(step, 4)), 4)
-            pz = lax.rem(z + away(lax.rem(step, 4)), 4)
-            prow = py * 4 + pz
-            for far in (2, 1, 3, 0):
-                act(prow, peer_cols[far], peer_cols[far] * 16 + prow)
-            return carry
-
-        lax.fori_loop(0, 15, rows_step, 0)
-        for far in (2, 1, 3):
-            act(row, peer_cols[far], peer_cols[far] * 16 + row)
+        for dx, dy, dz in FAR_FIRST:
+            prow = peer_ys[dy] + peer_zs[dz]
+            act(prow, peer_cols[dx], peer_cols[dx] * 16 + prow)
 
     barrier = pltpu.get_barrier_semaphore()
 

time: 58.7 us -> 57.8 us (0.985)
  Pallas kernels: 57.7 us -> 56.7 us
    pallas_call x1, Pallas kernels: 57.7 us -> 56.7 us  [per_device(): pl.pallas_call(kernel, out_shape=pltpu.VMEM(trunk.shape, BF16), in_specs=...]
where the time goes in v5:
time: 57.8 us; the launch traced here: 57.7 us
  Pallas kernels  56.7 us (98%)
  local copies, waits for them, and re-layouts  0.97 us (2%)
    pallas_call x1, Pallas kernels, per_device(): pl.pallas_call(kernel, out_shape=pltpu.VMEM(trunk.shape, BF16), in_specs=...  56.7 us

profile of v5, /device:TPU:1, one launch (start us, length us, event | category | flops | bytes accessed | tf_op | source)
XLA Modules:
  0.0 57.7 jit_solution(7921797627998254285)
XLA Ops:
  0.0 56.7 %template_block.1 = bf16[32,128,128]{2,1,0:T(8,128)(2,1)S(1)} custom-call(bf16[1,32,64,128]{3,2,1,0:T(8,128)(2,1)} %tp_hbm.1, bf16[32,128,128]{2,1,0:T(8,128)(2,1)} %trunk_hbm.1, s32[2,512]{1,0:T(2,128)} %cover_hbm.1, s32[1,512]{1,0:T(1,128)} %bitcast.3, f32[64]{0:T(128)} %vec_hbm.1, bf16[64,128]{1,0:T(8,128)(2,1)} %wt_hbm.1, bf16[2,5,64,64]{3,2,1,0:T(8,128)(2,1)} %wp_hbm.1, ...), custom_call_target="tpu_custom_call" | custom-call | tf_op jit(solution)/shard_map/template_block/pallas_call | solution.py:391
  56.7 1.0 %copy.11 = bf16[32,128,128]{2,1,0:T(8,128)(2,1)} copy(bf16[32,128,128]{2,1,0:T(8,128)(2,1)S(1)} %template_block.1) | data formatting | bytes 2097152

commit v6 on v5

--- a/solution.py
+++ b/solution.py
@@ -64,7 +64,7 @@
     out_v,
     cover_ref, chain_ref, vec_ref, wt_ref, wp_ref, wo_ref, wf_ref, tp_v, tr_v, vec_v, diag_v, k_perm, k_trunk, k_proj, k_out, k_final, k_lane,
     pair_v, normed_v, gate_v, sbuf, rbuf, tsend, tbuf, psend, pbuf,
-    ld_sem, own_sem, ssem, rsem, tssem, trsem, pssem, prsem,
+    ld_sem, own_sem, ssem, rsem, tssem, trsem, pssem, prsem, lsem,
 ):
     tmpl = lax.axis_index("tmpl")
     row = lax.axis_index("row")
@@ -145,7 +145,7 @@
     cols_of = cover_ref[:, lanes].astype(F32)
     masks = [row_plane(cover[t : t + 1]) * cols_of[t : t + 1] for t in range(2)]
     mask = jnp.where(tmpl == 0, masks[0], masks[1])
-    count = jnp.maximum(masks[0] + masks[1], 1.0)
+    share = 1.0 / jnp.maximum(masks[0] + masks[1], 1.0)
     chain_rows = row_plane(chain_ref[...].astype(F32))
     same_chain = jnp.where(chain_rows == chain_ref[:, lanes].astype(F32), 1.0, 0.0)
 
@@ -184,6 +184,12 @@
         tri_norm = to_rhs(norm0(tri))
         update = gate_v[h] * from_out(dot(k_out[m], tri_norm))
         return (pair_v[h].astype(F32) + update).astype(BF16)
+
+    def eighth(ref, number, e):
+        return ref.at[0, number, 0, pl.ds(e * 8, 8), :]
+
+    def tri_rows(ref, number, e):
+        return ref.at[0, number, pl.ds(e * 8, 8), :]
 
     def send_side(m, side, h):
         send_all(
@@ -226,7 +232,11 @@
         k_proj[0, d] = kron8(wp_ref[0, d])
     for h in range(2):
         product(0, 0, h)
-        send_side(0, 0, h)
+        for e in (2 * h, 2 * h + 1):
+            send_all(
+                lambda n: eighth(sbuf, n, e), eighth(rbuf, me, e),
+                lsem.at[0, e], lsem.at[1, e], lsem.at[2, e],
+            )
 
 
     k_proj[0, 4] = kron8(wp_ref[0, 4])
@@ -261,21 +271,28 @@
     right = jnp.concatenate(
         [rbuf[0, q * 16 : (q + 1) * 16, 1].reshape(512, COLS) for q in range(4)], axis=1
     )
-    for h in range(2):
-        lo = h * HALF
-        wait_side(0, 0, h)
+    for e in range(4):
+        lo = e * 8
+        wait_all(rbuf.at[0, pl.ds(0, DEV - 1), 0, pl.ds(lo, 8), :], lsem.at[1, e])
+        pltpu.make_async_copy(eighth(sbuf, me, e), eighth(rbuf, me, e), lsem.at[2, e]).wait()
         left = jnp.concatenate(
-            [rbuf[0, q * 16 : (q + 1) * 16, 0, lo : lo + HALF].reshape(256, COLS) for q in range(4)],
+            [rbuf[0, q * 16 : (q + 1) * 16, 0, lo : lo + 8].reshape(128, COLS) for q in range(4)],
             axis=1,
         )
         tri = lax.dot_general(left, right, (((1,), (1,)), ((), ())), preferred_element_type=F32)
         for q in range(4):
-            tsend[0, q * 16 : (q + 1) * 16, lo : lo + HALF, :] = (
-                tri[:, q * COLS : (q + 1) * COLS].reshape(16, HALF, COLS).astype(BF16)
+            tsend[0, q * 16 : (q + 1) * 16, lo : lo + 8, :] = (
+                tri[:, q * COLS : (q + 1) * COLS].reshape(16, 8, COLS).astype(BF16)
             )
-        send_tri(0, h)
-    for h in range(2):
-        pair = updated(0, h, wait_tri(0, h))
+        send_all(
+            lambda n: tri_rows(tsend, n, e), tri_rows(tbuf, me, e),
+            lsem.at[3, e], lsem.at[4, e], lsem.at[5, e],
+        )
+    for h in range(2):
+        for e in (2 * h, 2 * h + 1):
+            wait_all(tbuf.at[0, pl.ds(0, DEV - 1), pl.ds(e * 8, 8), :], lsem.at[4, e])
+            pltpu.make_async_copy(tri_rows(tsend, me, e), tri_rows(tbuf, me, e), lsem.at[5, e]).wait()
+        pair = updated(0, h, tbuf[0, :, h * HALF : (h + 1) * HALF, :].astype(F32))
         pair_v[h] = pair
         normed_v[h] = to_rhs(norm0(pair.astype(F32)))
         product(1, 1, h)
@@ -334,7 +351,7 @@
         across(h).wait_recv()
         lo = h * HALF
         total = psend[h].astype(F32) + pbuf[h].astype(F32)
-        hidden = jnp.maximum(total / count[lo : lo + HALF][None], 0.0)
+        hidden = jnp.maximum(total * share[lo : lo + HALF][None], 0.0)
         out = dot(k_final[...], to_rhs(hidden))
         for side in range(2):
             first = lo + 8 * side
@@ -343,10 +360,13 @@
 
     for h in range(2):
         across(h).wait_send()
-        for m in range(2):
-            for side in range(2):
-                wait_all(sbuf.at[m, pl.ds(0, DEV - 1), side, half(h), :], ssem.at[m, side, h])
-            wait_all(tsend.at[m, pl.ds(0, DEV - 1), half(h), :], tssem.at[m, h])
+        wait_all(sbuf.at[0, pl.ds(0, DEV - 1), 1, half(h), :], ssem.at[0, 1, h])
+        for side in range(2):
+            wait_all(sbuf.at[1, pl.ds(0, DEV - 1), side, half(h), :], ssem.at[1, side, h])
+        wait_all(tsend.at[1, pl.ds(0, DEV - 1), half(h), :], tssem.at[1, h])
+    for e in range(4):
+        wait_all(sbuf.at[0, pl.ds(0, DEV - 1), 0, pl.ds(e * 8, 8), :], lsem.at[0, e])
+        wait_all(tsend.at[0, pl.ds(0, DEV - 1), pl.ds(e * 8, 8), :], lsem.at[3, e])
 
 
 def per_device(tp, trunk, coverage, chain_ids, chain_vec, wt, wp, wo, wf):
@@ -387,6 +407,7 @@
         pltpu.SemaphoreType.DMA((2, 2)),
         pltpu.SemaphoreType.DMA((2,)),
         pltpu.SemaphoreType.DMA((2,)),
+        pltpu.SemaphoreType.DMA((6, 4)),
     ]
     return pl.pallas_call(
         kernel,

time: 57.8 us -> 57 us (0.986)
  Pallas kernels: 56.7 us -> 55.9 us
    pallas_call x1, Pallas kernels: 56.7 us -> 55.9 us  [per_device(): pl.pallas_call(kernel, out_shape=pltpu.VMEM(trunk.shape, BF16), in_specs=...]
where the time goes in v6:
time: 57 us; the launch traced here: 56.9 us
  Pallas kernels  55.9 us (98%)
  local copies, waits for them, and re-layouts  0.97 us (2%)
    pallas_call x1, Pallas kernels, per_device(): pl.pallas_call(kernel, out_shape=pltpu.VMEM(trunk.shape, BF16), in_specs=...  55.9 us

profile of v6, /device:TPU:1, one launch (start us, length us, event | category | flops | bytes accessed | tf_op | source)
XLA Modules:
  0.0 56.9 jit_solution(8235360245172909256)
XLA Ops:
  0.0 55.9 %template_block.1 = bf16[32,128,128]{2,1,0:T(8,128)(2,1)S(1)} custom-call(bf16[1,32,64,128]{3,2,1,0:T(8,128)(2,1)} %tp_hbm.1, bf16[32,128,128]{2,1,0:T(8,128)(2,1)} %trunk_hbm.1, s32[2,512]{1,0:T(2,128)} %cover_hbm.1, s32[1,512]{1,0:T(1,128)} %bitcast.3, f32[64]{0:T(128)} %vec_hbm.1, bf16[64,128]{1,0:T(8,128)(2,1)} %wt_hbm.1, bf16[2,5,64,64]{3,2,1,0:T(8,128)(2,1)} %wp_hbm.1, ...), custom_call_target="tpu_custom_call" | custom-call | tf_op jit(solution)/shard_map/template_block/pallas_call | solution.py:412
  55.9 1.0 %copy.11 = bf16[32,128,128]{2,1,0:T(8,128)(2,1)} copy(bf16[32,128,128]{2,1,0:T(8,128)(2,1)S(1)} %template_block.1) | data formatting | bytes 2097152
